TPU v7x, 128 devices: a whole 4x4x4 slice. The times are simulated.
128 devices in a mesh: mem: 16 (over y, x), pix: 8 (over z, core).
Axes of the slice: x: 4, y: 4, z: 4, core: 2. Of those that a mesh axis runs over, the one named last changes fastest.
Arguments:
- prior_motion: bfloat16 [64, 16, 262144], P('mem', None, 'pix'), may hold values from -6 to 6
- measured_motion: float32 [1200], replicated, may hold values from -1.6 to 1.6
- measurement_noise_stddev: float32 [1200], replicated, may hold values from 0.05 to 0.5
- gaussian_jitter: float32 [2, 1200, 64], replicated, may hold values from -6 to 6
- scene_couples: int32 [2, 1200], replicated, may hold values from 0 to 15, as said below
- targeted_tile_number: int32 [1200], replicated, may hold values from 0 to 4095
Outputs:
- analysis: bfloat16 [64, 16, 262144], P('mem', None, 'pix')
Inputs may be any that keep to these rules, and one draw needn't show every extreme that they name: scene_couples[0, k] < scene_couples[1, k]: row 0 holds the earlier acquisition, row 1 the later.
All inputs are finite; a program needn't handle non-finite values.
Results may differ from a plain program's by a relative error of at most 0.011.
Values may be sent and summed in bfloat16 or wider, within the bound.
A program may use at most 128 MiB of HBM per device.

v0:
```python
import math
import jax
import jax.numpy as jnp
from jax import lax
from jax.sharding import PartitionSpec as P

BLK = 64
PASS_COUNT = 2


def block_sums(pieces):
    part_cells = pieces.shape[2]
    block_count = part_cells // BLK
    summer = (
        jnp.arange(part_cells, dtype=jnp.int32)[:, None] // BLK
        == jnp.arange(block_count, dtype=jnp.int32)[None, :]
    ).astype(jnp.bfloat16)
    flat = jnp.dot(pieces.reshape(-1, part_cells), summer, preferred_element_type=jnp.float32)
    return flat.reshape(pieces.shape[0], pieces.shape[1], block_count)


def with_sums(pieces):
    return (pieces, block_sums(pieces))


def to_pixels(ground_motion_vector):
    return with_sums(
        lax.all_to_all(ground_motion_vector, "mem", split_axis=2, concat_axis=0, tiled=True)
    )


def to_members(pixel_state):
    return lax.all_to_all(pixel_state, "mem", split_axis=0, concat_axis=2, tiled=True)


def predict(sums, picker):
    flat_sums = sums.reshape(sums.shape[0], -1)
    return (
        jnp.dot(
            picker, flat_sums.T, precision=lax.Precision.HIGHEST, preferred_element_type=jnp.float32
        )
        / BLK
    )


def member_terms(predicted, measured_motion, member_anomaly, noise):
    realization_vectors = predicted.shape[1]
    centred = predicted - jnp.mean(predicted, axis=1, keepdims=True)
    scaled = centred / (member_anomaly[:, None] * math.sqrt(realization_vectors - 1))
    misfit = (
        measured_motion[:, None] + member_anomaly[:, None] * noise - predicted
    ) / member_anomaly[:, None]
    return (scaled, misfit)


def products(scaled, misfit):
    gram = jnp.dot(
        scaled.T, scaled, precision=lax.Precision.HIGHEST, preferred_element_type=jnp.float32
    )
    cross = jnp.dot(
        scaled.T, misfit, precision=lax.Precision.HIGHEST, preferred_element_type=jnp.float32
    )
    return (gram, cross)


def solve_mixing(gram, cross):
    realization_vectors = gram.shape[0]
    factor = jnp.linalg.cholesky(jnp.eye(realization_vectors, dtype=jnp.float32) + gram)
    return (
        jax.scipy.linalg.cho_solve((factor, True), cross) / math.sqrt(realization_vectors - 1)
    ).astype(jnp.bfloat16)


def update(pixel_state, mixing):
    realization_vectors = pixel_state.shape[0]
    average = jnp.sum(pixel_state, axis=0, dtype=jnp.float32) / realization_vectors
    anomaly = (pixel_state.astype(jnp.float32) - average).astype(jnp.bfloat16)
    change = jnp.dot(
        mixing.T, anomaly.reshape(realization_vectors, -1), preferred_element_type=jnp.float32
    )
    return (pixel_state.astype(jnp.float32) + change.reshape(pixel_state.shape)).astype(
        jnp.bfloat16
    )


def body(
    prior_motion,
    measured_motion,
    measurement_noise_stddev,
    gaussian_jitter,
    scene_couples,
    targeted_tile_number,
):
    cells_per_tile = prior_motion.shape[2]
    part_width = cells_per_tile // lax.axis_size("mem")
    local_blocks = part_width // BLK
    first_block = (
        lax.axis_index("pix") * cells_per_tile + lax.axis_index("mem") * part_width
    ) // BLK
    block_range = first_block + jnp.arange(local_blocks, dtype=jnp.int32)
    block_table = (targeted_tile_number[:, None] == block_range[None, :]).astype(jnp.float32)
    scene_timeline = jnp.arange(prior_motion.shape[1], dtype=jnp.int32)
    pair_table = (scene_timeline[None, :] == scene_couples[1][:, None]).astype(jnp.float32) - (
        scene_timeline[None, :] == scene_couples[0][:, None]
    ).astype(jnp.float32)
    picker = (pair_table[:, :, None] * block_table[:, None, :]).reshape(pair_table.shape[0], -1)
    member_anomaly = jnp.sqrt(jnp.float32(float(PASS_COUNT))) * measurement_noise_stddev
    pixel_state, sums = to_pixels(prior_motion)
    for iteration in range(PASS_COUNT):
        if iteration > 0:
            sums = block_sums(pixel_state)
        predicted = predict(sums, picker)
        scaled, misfit = member_terms(
            predicted, measured_motion, member_anomaly, gaussian_jitter[iteration]
        )
        gram, cross = lax.psum(products(scaled, misfit), ("mem", "pix"))
        pixel_state = update(pixel_state, solve_mixing(gram, cross))
    return to_members(pixel_state)


def solution(mesh):
    return jax.shard_map(
        body,
        mesh=mesh,
        in_specs=(P("mem", None, "pix"), P(), P(), P(), P(), P()),
        out_specs=P("mem", None, "pix"),
        check_vma=False,
    )
```

profile of v0, /device:TPU:0, one launch (start us, length us, event | category | flops | bytes accessed | tf_op | source)
XLA Modules:
  0.0 537.7 jit_solution(16468579744521945431)
XLA Ops:
  0.0 37.7 %copy.41 = bf16[4,16,32768]{1,0,2:T(4,128)(2,1)} copy(bf16[4,16,32768]{2,1,0:T(8,128)(2,1)} %param.9) | data formatting | bytes 8388608 | tf_op args[0]
  37.7 36.8 %reshape.195 = bf16[16,2,65536]{2,1,0:T(2,128)(2,1)} reshape(bf16[32768,4,16]{2,1,0:T(4,128)(2,1)} %bitcast.107) | data formatting | bytes 8388608
  74.6 7.3 %all-to-all-start = ((bf16[16,2,65536]{2,1,0:T(2,128)(2,1)}), bf16[16,2,65536]{2,1,0:T(2,128)(2,1)}, u32[]{:S(2)}, u32[]{:S(2)}) async-start(bf16[16,2,65536]{2,1,0:T(2,128)(2,1)} %reshape.195), calls=%async_computation | async-start | bytes 8388608 | tf_op jit(solution)/shard_map/all_to_all | solution.py:28
  82.1 0.2 broadcast_multiply_fusion
  82.4 62.8 %all-to-all-done = bf16[16,2,65536]{2,1,0:T(2,128)(2,1)} async-done(((bf16[16,2,65536]{2,1,0:T(2,128)(2,1)}), bf16[16,2,65536]{2,1,0:T(2,128)(2,1)}, u32[]{:S(2)}, u32[]{:S(2)}) %all-to-all-start) | async-done | bytes 4194336 | tf_op jit(solution)/shard_map/all_to_all | solution.py:28
  145.2 25.6 %reshape.196 = bf16[32768,4,16]{2,1,0:T(4,128)(2,1)} reshape(bf16[16,2,65536]{2,1,0:T(2,128)(2,1)} %all-to-all-done) | data formatting | bytes 8388608
  170.8 44.3 %copy.66 = bf16[4,16,16,2048]{3,1,0,2:T(8,128)(2,1)} copy(bf16[4,16,16,2048]{1,0,3,2:T(4,128)(2,1)} %bitcast.105) | data formatting | bytes 8388608 | tf_op jit(solution)/shard_map/all_to_all | solution.py:28
  215.1 33.7 %copy.65 = bf16[4,16,16,2048]{3,2,1,0:T(8,128)(2,1)} copy(bf16[4,16,16,2048]{1,0,3,2:T(4,128)(2,1)} %bitcast.106) | data formatting | bytes 8388608 | tf_op jit(solution)/shard_map/all_to_all | solution.py:28
  248.9 3.4 bitcast_convert_fusion
  252.3 0.9 fusion.7
  253.2 2.3 copy-done
  255.5 8.1 %copy.48 = f32[16,4,16,2048]{3,2,1,0:T(8,128)} copy(f32[16,4,16,2048]{3,0,2,1:T(8,128)S(1)} %bitcast_convert_fusion) | data formatting | bytes 16777216 | tf_op jit(solution)/shard_map/convert_element_type | solution.py:81
  263.6 12.4 %copy.43 = f32[16,4,16,2048]{3,1,0,2:T(4,128)} copy(f32[16,4,16,2048]{3,0,2,1:T(8,128)} %copy-done) | data formatting | bytes 16777216 | tf_op jit(solution)/shard_map/convert_element_type | solution.py:81
  276.0 3.5 convolution_bitcast_fusion
  279.6 0.2 copy.45
  279.8 0.2 reshape_reshape.6
  280.0 1.8 fusion.56
  281.8 0.4 fusion.29
  282.3 0.5 fusion.25
  282.8 65.0 %all-reduce.1 = (f32[64,64]{1,0:T(8,128)S(1)}, f32[64,64]{0,1:T(8,128)S(1)}) all-reduce(f32[64,64]{1,0:T(8,128)S(1)} %fusion.25, f32[64,64]{0,1:T(8,128)S(1)} %fusion.29), channel_id=1, replica_groups=mesh['mem'=16,'pix'=8] {'mem','pix'}, use_global_device_ids=true, to_apply=%region_4.6 | all-reduce | flops 8192 | bytes 65536 | tf_op jit(solution)/shard_map/psum | solution.py:116
  347.9 5.8 %cholesky.44 = f32[64,64]{1,0:T(8,128)S(1)} custom-call(f32[64,64]{1,0:T(8,128)S(1)} %fusion.52), custom_call_target="Cholesky" | custom-call | tf_op jit(solution)/shard_map/jit(cholesky)/cholesky | solution.py:68
  353.8 0.6 compare_reduce_fusion.1
  354.4 0.7 fusion.43
  355.1 4.9 custom-call.8
  360.0 0.3 fusion.50
  360.2 0.2 fusion.11
  360.4 11.6 %copy.73 = f32[8,8,16,2048]{3,1,2,0:T(8,128)} copy(f32[8,8,16,2048]{3,2,1,0:T(8,128)} %bitcast.108) | data formatting | bytes 16777216
  372.1 10.2 %reshape.189 = f32[64,16,2048]{2,0,1:T(8,128)} reshape(f32[16,4,16,2048]{3,1,0,2:T(4,128)} %copy.43) | data formatting | bytes 16777216 | tf_op jit(solution)/shard_map/convert_element_type | solution.py:81
  382.3 4.1 subtract_convert_fusion
  386.4 1.7 copy-done.2
  388.1 1.4 convert_reduce_fusion
  389.5 2.3 copy.51
  391.8 1.4 fusion.12
  393.2 0.2 reshape_reshape.7
  393.4 1.8 fusion.57
  395.2 0.4 fusion.30
  395.6 0.5 fusion.20
  396.1 64.4 %all-reduce = (f32[64,64]{1,0:T(8,128)S(1)}, f32[64,64]{0,1:T(8,128)S(1)}) all-reduce(f32[64,64]{1,0:T(8,128)S(1)} %fusion.20, f32[64,64]{0,1:T(8,128)S(1)} %fusion.30), channel_id=1, replica_groups=mesh['mem'=16,'pix'=8] {'mem','pix'}, use_global_device_ids=true, to_apply=%region_8.11 | all-reduce | flops 8192 | bytes 65536 | tf_op jit(solution)/shard_map/psum | solution.py:116
  460.7 5.8 %cholesky.55 = f32[64,64]{1,0:T(8,128)S(1)} custom-call(f32[64,64]{1,0:T(8,128)S(1)} %fusion.48), custom_call_target="Cholesky" | custom-call | tf_op jit(solution)/shard_map/jit(cholesky)/cholesky | solution.py:68
  466.5 0.7 compare_reduce_fusion
  467.3 0.7 fusion.44
  468.0 4.9 custom-call.9
  472.9 0.3 fusion.46
  473.1 0.2 fusion.10
  473.3 5.0 fusion.1
  478.4 2.3 copy.58
  480.7 54.4 %all_to_all.33 = bf16[64,16,2048]{2,1,0:T(8,128)(2,1)S(1)} all-to-all(bf16[64,16,2048]{2,1,0:T(8,128)(2,1)S(1)} %copy.58), channel_id=1, replica_groups=mesh['mem'=16,'pix'=8] {'mem'}, dimensions={0} | all-to-all | bytes 8388608 | tf_op jit(solution)/shard_map/all_to_all | solution.py:33
  535.1 2.3 copy.72
  (36 shorter events, 0.5 us)
Async XLA Ops:
  74.6 7.4 %copy-start.4 = (s32[2,1200]{1,0:T(2,128)S(1)}, s32[2,1200]{1,0:T(2,128)}, u32[]{:S(2)}) copy-start(s32[2,1200]{1,0:T(2,128)} %param.13) | copy-start | bytes 28804
  74.6 7.5 %copy-start.6 = (s32[1200]{0:T(1024)S(1)}, s32[1200]{0:T(1024)}, u32[]{:S(2)}) copy-start(s32[1200]{0:T(1024)} %param.14) | copy-start | bytes 14404
  74.6 70.6 %all-to-all-start = ((bf16[16,2,65536]{2,1,0:T(2,128)(2,1)}), bf16[16,2,65536]{2,1,0:T(2,128)(2,1)}, u32[]{:S(2)}, u32[]{:S(2)}) async-start(bf16[16,2,65536]{2,1,0:T(2,128)(2,1)} %reshape.195), calls=%async_computation | async-start | bytes 8388608 | tf_op jit(solution)/shard_map/all_to_all | solution.py:28
  248.9 3.5 copy-start.1
  252.3 3.2 copy-start
  276.0 5.8 %copy-start.5 = (f32[1200]{0:T(1024)S(1)}, f32[1200]{0:T(1024)}, u32[]{:S(2)}) copy-start(f32[1200]{0:T(1024)} %param.11) | copy-start | bytes 14404
  276.0 6.3 %copy-start.9 = (f32[1200]{0:T(1024)S(1)}, f32[1200]{0:T(1024)}, u32[]{:S(2)}) copy-start(f32[1200]{0:T(1024)} %param.10) | copy-start | bytes 14404
  280.0 2.3 copy-start.7
  382.3 5.8 %copy-start.2 = (f32[64,16,2048]{2,0,1:T(8,128)S(1)}, f32[64,16,2048]{2,0,1:T(8,128)}, u32[]{:S(2)}) copy-start(f32[64,16,2048]{2,0,1:T(8,128)} %reshape.189) | copy-start | bytes 25165828
  389.5 2.3 copy-start.3
  393.4 2.2 copy-start.8
where the time goes:
time: 546 us; the launch traced here: 538 us
  local copies, waits for them, and re-layouts  232 us (42%)
  blocking collectives  184 us (34%)
  waiting for transfers between devices  62.8 us (12%)
  other arithmetic  33.1 us (6%)
  matrix products  17.5 us (3%)
  starting transfers between devices  7.33 us (1%)
    psum x2, blocking collectives, body(): gram, cross = lax.psum(products(scaled, misfit), ('mem', 'pix'))  129 us
    unnamed x25, local copies, waits for them, and re-layouts  116 us
    all_to_all x2, local copies, waits for them, and re-layouts, to_pixels(): lax.all_to_all(ground_motion_vector, 'mem', split_axis=2, concat_axis=0,...  78.1 us
    all_to_all x1, waiting for transfers between devices, to_pixels(): lax.all_to_all(ground_motion_vector, 'mem', split_axis=2, concat_axis=0,...  62.8 us
    all_to_all x1, blocking collectives, to_members(): lax.all_to_all(pixel_state, 'mem', split_axis=0, concat_axis=2, tiled=True)  54.4 us
    convert_element_type x3, local copies, waits for them, and re-layouts, update(): pixel_state.astype(jnp.float32) + change.reshape(pixel_state.shape)  30.7 us
    another operation x6, other arithmetic, solve_mixing(): jnp.linalg.cholesky(jnp.eye(realization_vectors, dtype=jnp.float32) + gram)  13.1 us
    another operation x4, other arithmetic, solve_mixing(): jax.scipy.linalg.cho_solve((factor, True), cross)  11.1 us
  transfers between devices with their start and end apart: 1, of which 1 were waited for; matrix products, arithmetic and copies ran while one was open for 0% of the time, Pallas kernels for 0%

commit v1 on v0

--- a/solution.py
+++ b/solution.py
@@ -6,6 +6,13 @@
 
 BLK = 64
 PASS_COUNT = 2
+
+
+def set_pipes(frame):
+    return jnp.concatenate(
+        lax.all_to_all(jnp.stack(jnp.split(frame, lax.axis_size("mem"), axis=2)), "mem", 0, 0),
+        axis=0,
+    )
 
 
 def block_sums(pieces):
@@ -24,9 +31,7 @@
 
 
 def to_pixels(ground_motion_vector):
-    return with_sums(
-        lax.all_to_all(ground_motion_vector, "mem", split_axis=2, concat_axis=0, tiled=True)
-    )
+    return with_sums(set_pipes(ground_motion_vector))
 
 
 def to_members(pixel_state):

time: 546 us -> 354 us (0.65); the launches traced: 538 us -> 353 us
  local copies, waits for them, and re-layouts: 232 us -> 39.4 us
  matrix products: 17.5 us -> 25.6 us
    unnamed x25 -> x29, local copies, waits for them, and re-layouts: 116 us -> 30.1 us
    all_to_all x2 -> x0, local copies, waits for them, and re-layouts: 78.1 us -> none  [to_pixels(): lax.all_to_all(ground_motion_vector, 'mem', split_axis=2, concat_axis=0,...]
    convert_element_type x3 -> x0, local copies, waits for them, and re-layouts: 30.7 us -> none  [update(): pixel_state.astype(jnp.float32) + change.reshape(pixel_state.shape)]
    dot_general x2, matrix products: 6.43 us -> 13.5 us  [update(): jnp.dot(mixing.T, anomaly.reshape(realization_vectors, -1), preferred_ele...]
where the time goes in v1:
time: 354 us; the launch traced here: 353 us
  blocking collectives  184 us (52%)
  waiting for transfers between devices  62.8 us (18%)
  local copies, waits for them, and re-layouts  39.4 us (11%)
  other arithmetic  33.4 us (9%)
  matrix products  25.6 us (7%)
  starting transfers between devices  7.33 us (2%)
    psum x2, blocking collectives, body(): gram, cross = lax.psum(products(scaled, misfit), ('mem', 'pix'))  129 us
    all_to_all x1, waiting for transfers between devices, set_pipes(): lax.all_to_all(jnp.stack(jnp.split(frame, lax.axis_size('mem'), axis=2)),...  62.8 us
    all_to_all x1, blocking collectives, to_members(): lax.all_to_all(pixel_state, 'mem', split_axis=0, concat_axis=2, tiled=True)  54.6 us
    unnamed x29, local copies, waits for them, and re-layouts  30.1 us
    dot_general x2, matrix products, update(): jnp.dot(mixing.T, anomaly.reshape(realization_vectors, -1), preferred_ele...  13.5 us
    another operation x6, other arithmetic, solve_mixing(): jnp.linalg.cholesky(jnp.eye(realization_vectors, dtype=jnp.float32) + gram)  13.1 us
    another operation x4, other arithmetic, solve_mixing(): jax.scipy.linalg.cho_solve((factor, True), cross)  11.1 us
    all_to_all x1, starting transfers between devices, set_pipes(): lax.all_to_all(jnp.stack(jnp.split(frame, lax.axis_size('mem'), axis=2)),...  7.33 us
  transfers between devices with their start and end apart: 1, of which 1 were waited for; matrix products, arithmetic and copies ran while one was open for 0% of the time, Pallas kernels for 0%

profile of v1, /device:TPU:0, one launch (start us, length us, event | category | flops | bytes accessed | tf_op | source)
XLA Modules:
  0.0 352.7 jit_solution(8685204180886014605)
XLA Ops:
  0.0 1.7 bitcast_dynamic-update-slice_fusion.15
  1.7 1.7 bitcast_dynamic-update-slice_fusion.14
  3.3 1.7 bitcast_dynamic-update-slice_fusion.13
  5.0 1.7 bitcast_dynamic-update-slice_fusion.12
  6.7 1.7 bitcast_dynamic-update-slice_fusion.11
  8.3 1.7 bitcast_dynamic-update-slice_fusion.10
  10.0 1.7 bitcast_dynamic-update-slice_fusion.9
  11.7 1.7 bitcast_dynamic-update-slice_fusion.8
  13.4 1.7 bitcast_dynamic-update-slice_fusion.7
  15.0 1.7 bitcast_dynamic-update-slice_fusion.6
  16.7 1.7 bitcast_dynamic-update-slice_fusion.5
  18.4 1.7 bitcast_dynamic-update-slice_fusion.4
  20.0 1.7 bitcast_dynamic-update-slice_fusion.3
  21.7 1.7 bitcast_dynamic-update-slice_fusion.2
  23.4 1.7 bitcast_dynamic-update-slice_fusion.1
  25.0 1.7 bitcast_dynamic-update-slice_fusion
  26.7 7.3 %all-to-all-start = ((bf16[16,4,16,2048]{3,2,1,0:T(8,128)(2,1)}), bf16[16,4,16,2048]{3,2,1,0:T(8,128)(2,1)}, u32[]{:S(2)}, u32[]{:S(2)}) async-start(bf16[16,4,16,2048]{3,2,1,0:T(8,128)(2,1)} %bitcast_dynamic-update-slice_fusion), calls=%async_computation | async-start | bytes 8388608 | tf_op jit(solution)/shard_map/all_to_all | solution.py:13
  34.5 62.8 %all-to-all-done = bf16[16,4,16,2048]{3,2,1,0:T(8,128)(2,1)} async-done(((bf16[16,4,16,2048]{3,2,1,0:T(8,128)(2,1)}), bf16[16,4,16,2048]{3,2,1,0:T(8,128)(2,1)}, u32[]{:S(2)}, u32[]{:S(2)}) %all-to-all-start) | async-done | bytes 4194336 | tf_op jit(solution)/shard_map/all_to_all | solution.py:13
  97.3 2.9 convert_reduce_fusion.1
  100.3 3.6 %fusion.13 = f32[1024,32]{1,0:T(8,128)S(1)} fusion(bf16[1024,2048]{1,0:T(8,128)(2,1)} %bitcast.18, s32[2048]{0:T(1024)S(1)} %add_select_fusion), kind=kOutput, calls=%fused_computation.25 | convolution fusion | flops 134283264 | bytes 4333568 | tf_op jit(solution)/shard_map/dot_general | solution.py:25
  104.1 1.8 fusion.55
  105.9 0.4 fusion.28
  106.3 0.5 fusion.24
  106.8 65.2 %all-reduce.1 = (f32[64,64]{1,0:T(8,128)S(1)}, f32[64,64]{0,1:T(8,128)S(1)}) all-reduce(f32[64,64]{1,0:T(8,128)S(1)} %fusion.24, f32[64,64]{0,1:T(8,128)S(1)} %fusion.28), channel_id=1, replica_groups=mesh['mem'=16,'pix'=8] {'mem','pix'}, use_global_device_ids=true, to_apply=%region_4.6 | all-reduce | flops 8192 | bytes 65536 | tf_op jit(solution)/shard_map/psum | solution.py:121
  172.1 5.8 %cholesky.44 = f32[64,64]{1,0:T(8,128)S(1)} custom-call(f32[64,64]{1,0:T(8,128)S(1)} %fusion.51), custom_call_target="Cholesky" | custom-call | tf_op jit(solution)/shard_map/jit(cholesky)/cholesky | solution.py:73
  178.0 0.6 compare_reduce_fusion.1
  178.6 0.7 fusion.42
  179.3 4.9 %custom-call.8 = f32[1,64,64]{1,2,0:T(8,128)S(1)} custom-call(f32[1,64,64]{2,1,0:T(8,128)S(1)} %fusion.42), custom_call_target="InvertDiagBlocksLowerTriangular" | custom-call | tf_op jit(solution)/shard_map/jit(_cho_solve)/triangular_solve | solution.py:75
  184.2 0.3 fusion.49
  184.6 3.3 convert_element_type.86
  187.9 5.0 %copy.53 = f32[8,8,16,2048]{3,1,2,0:T(8,128)S(1)} copy(f32[8,8,16,2048]{3,2,1,0:T(8,128)S(1)} %bitcast.125) | data formatting | bytes 16777216
  192.9 2.6 subtract_convert_fusion
  195.5 8.5 %convert_reduce_fusion = (f32[16,2048]{1,0:T(8,128)S(1)}, bf16[64,16,2048]{2,0,1:T(8,128)(2,1)S(1)}) fusion(bf16[64,64,1]{1,0,2:T(8,128)(2,1)S(1)} %fusion.11, bf16[8,16,8,2048]{3,2,1,0:T(8,128)(2,1)} %bitcast.130, f32[64,16,2048]{2,1,0:T(8,128)S(1)} %bitcast.126), kind=kOutput, calls=%fused_computation.2 | convolution fusion | flops 276791296 | bytes 16916480 | tf_op jit(solution)/shard_map/dot_general | solution.py:83
  204.0 2.3 copy.31
  206.3 1.4 fusion.12
  208.0 1.8 fusion.56
  209.8 1.4 fusion.19
  211.2 0.4 fusion.29
  211.7 64.1 %all-reduce = (f32[64,64]{1,0:T(8,128)S(1)}, f32[64,64]{0,1:T(8,128)S(1)}) all-reduce(f32[64,64]{1,0:T(8,128)S(1)} %fusion.19, f32[64,64]{0,1:T(8,128)S(1)} %fusion.29), channel_id=1, replica_groups=mesh['mem'=16,'pix'=8] {'mem','pix'}, use_global_device_ids=true, to_apply=%region_8.11 | all-reduce | flops 8192 | bytes 65536 | tf_op jit(solution)/shard_map/psum | solution.py:121
  275.9 5.8 %cholesky.55 = f32[64,64]{1,0:T(8,128)S(1)} custom-call(f32[64,64]{1,0:T(8,128)S(1)} %fusion.47), custom_call_target="Cholesky" | custom-call | tf_op jit(solution)/shard_map/jit(cholesky)/cholesky | solution.py:73
  281.8 0.7 compare_reduce_fusion
  282.5 0.7 fusion.43
  283.2 4.9 %custom-call.9 = f32[1,64,64]{1,2,0:T(8,128)S(1)} custom-call(f32[1,64,64]{2,1,0:T(8,128)S(1)} %fusion.43), custom_call_target="InvertDiagBlocksLowerTriangular" | custom-call | tf_op jit(solution)/shard_map/jit(_cho_solve)/triangular_solve | solution.py:75
  288.1 0.3 fusion.45
  288.5 5.0 %fusion.1 = bf16[64,16,2048]{2,0,1:T(8,128)(2,1)S(1)} fusion(bf16[64,16,2048]{2,0,1:T(8,128)(2,1)} %copy-done, bf16[64,64,1]{1,0,2:T(8,128)(2,1)S(1)} %fusion.10, f32[16,2048]{1,0:T(8,128)S(1)} %broadcast_multiply_fusion.1), kind=kOutput, calls=%fused_computation.4 | convolution fusion | flops 281018368 | bytes 8527872 | tf_op jit(solution)/shard_map/dot_general | solution.py:83
  293.5 2.3 copy.38
  295.9 54.6 %all_to_all.23 = bf16[64,16,2048]{2,1,0:T(8,128)(2,1)S(1)} all-to-all(bf16[64,16,2048]{2,1,0:T(8,128)(2,1)S(1)} %copy.38), channel_id=1, replica_groups=mesh['mem'=16,'pix'=8] {'mem'}, dimensions={0} | all-to-all | bytes 8388608 | tf_op jit(solution)/shard_map/all_to_all | solution.py:38
  350.4 2.3 copy.52
  (35 shorter events, 1.5 us)
Async XLA Ops:
  26.7 7.4 %copy-start.1 = (s32[2,1200]{1,0:T(2,128)S(1)}, s32[2,1200]{1,0:T(2,128)}, u32[]{:S(2)}) copy-start(s32[2,1200]{1,0:T(2,128)} %param.13) | copy-start | bytes 28804
  26.7 7.5 %copy-start.3 = (s32[1200]{0:T(1024)S(1)}, s32[1200]{0:T(1024)}, u32[]{:S(2)}) copy-start(s32[1200]{0:T(1024)} %param.14) | copy-start | bytes 14404
  26.7 70.6 %all-to-all-start = ((bf16[16,4,16,2048]{3,2,1,0:T(8,128)(2,1)}), bf16[16,4,16,2048]{3,2,1,0:T(8,128)(2,1)}, u32[]{:S(2)}, u32[]{:S(2)}) async-start(bf16[16,4,16,2048]{3,2,1,0:T(8,128)(2,1)} %bitcast_dynamic-update-slice_fusion), calls=%async_computation | async-start | bytes 8388608 | tf_op jit(solution)/shard_map/all_to_all | solution.py:13
  100.2 5.6 %copy-start.2 = (f32[1200]{0:T(1024)S(1)}, f32[1200]{0:T(1024)}, u32[]{:S(2)}) copy-start(f32[1200]{0:T(1024)} %param.11) | copy-start | bytes 14404
  100.3 6.1 %copy-start.5 = (f32[1200]{0:T(1024)S(1)}, f32[1200]{0:T(1024)}, u32[]{:S(2)}) copy-start(f32[1200]{0:T(1024)} %param.10) | copy-start | bytes 14404
  104.1 2.3 copy-start.4
  204.0 2.3 copy-start
